TPU v7x, 128 devices: a whole 4x4x4 slice. The times are simulated.
128 devices in a mesh: grp: 4 (over z), wave: 32 (over x, y, core).
Axes of the slice: x: 4, y: 4, z: 4, core: 2. Of those that a mesh axis runs over, the one named last changes fastest.
Arguments:
- state: bfloat16 [275, 984320], P(None, ('grp', 'wave')), may hold values from -6 to 6
- held_orders: int32 [640], P(('grp', 'wave')), may hold values from -1 to 383, as said below
- pair_lows: int32 [384], P(('grp', 'wave')), may hold values from 0 to 383, each once
- inverses: bfloat16 [384, 2, 137, 137], P(('grp', 'wave')), may hold values from -2 to 3
- height_operator: bfloat16 [137, 137], replicated, may hold values from -0.5 to 0.5
- pressure_column: bfloat16 [137], replicated, may hold values from -5 to 5
- thermal_response_matrix: bfloat16 [137, 137], replicated, may hold values from -0.5 to 0.5
- mass_row: bfloat16 [137], replicated, may hold values from -0.5 to 0.5
Outputs:
- advanced: bfloat16 [275, 984320], P(None, ('grp', 'wave'))
Inputs may be any that keep to these rules, and one draw needn't show every extreme that they name: `held_orders`: each of 0 to 383 appears exactly once, all other entries are -1; some device has all 5 of its slots filled.
All inputs are finite; a program needn't handle non-finite values.
Results may differ from a plain program's by a relative error of at most 0.0052.
Values may be sent and summed in bfloat16 or wider, within the bound.
A program may use at most 128 MiB of HBM per device.

v0:
```python
import jax
import jax.numpy as jnp
from jax import lax
from jax.sharding import Mesh
from jax.sharding import PartitionSpec as P

GRP_WAVE = ("grp", "wave_0", "wave_1", "wave_2")
WAVE = ("wave_0", "wave_1", "wave_2")


def in_order(tiles, dim):
    shape = list(tiles.shape[1:])
    shape[dim] *= tiles.shape[0]
    return jnp.moveaxis(tiles, 0, dim).reshape(shape)


def all_blocks(shard, axes, turns):
    tiles = shard[None]
    for k in turns:
        tiles = lax.all_gather(tiles, axes[k], axis=0, tiled=True)
    held = [lax.axis_size(axes[k]) for k in reversed(turns)]
    tiles = tiles.reshape(*held, *shard.shape)
    turned = sorted(range(len(turns)), key=lambda place: turns[len(turns) - 1 - place])
    return tiles.transpose(*turned, *range(len(turns), tiles.ndim)).reshape(-1, *shard.shape)


def gathered_by_axis(shard, axes, turns, dim):
    return in_order(all_blocks(shard, axes, turns), dim)


def send_out(message):
    return lax.all_to_all(message, GRP_WAVE, split_axis=1, concat_axis=1, tiled=True)


def send_home(message):
    return lax.all_to_all(message, GRP_WAVE, split_axis=1, concat_axis=1, tiled=True)


def solve_columns(inverses, right_side, low_mask, split):
    upper = jnp.einsum(
        "jkl,lajc->kajc", inverses[:, 1], right_side, preferred_element_type=jnp.float32
    )
    lower = jnp.einsum(
        "jkl,lajc->kajc",
        inverses[:, 0],
        right_side[..., :split],
        preferred_element_type=jnp.float32,
    )
    first = jnp.where(low_mask[None, :, :, :split], lower, upper[..., :split])
    return jnp.concatenate([first, upper[..., split:]], axis=-1).astype(jnp.bfloat16)


def shards(
    state,
    held_orders,
    pair_lows,
    inverses,
    height_operator,
    pressure_column,
    thermal_response_matrix,
    mass_row,
):
    layer_heights_count = height_operator.shape[0]
    pair_count = pair_lows.shape[0]
    slot_count = held_orders.shape[0]
    devices = lax.axis_size("grp") * lax.axis_size(WAVE)
    truncation = 2 * pair_count * devices - 1
    slot_width = 2 * (truncation + 2)
    denom = float(truncation * (truncation + 1))
    fill_col = slot_count * slot_width
    all_lows = gathered_by_axis(pair_lows, (("grp", "wave_0", "wave_1"), "wave_2"), (0, 1), 0)
    own_low = pair_lows.reshape(1, pair_count, 1)
    all_orders = gathered_by_axis(held_orders, GRP_WAVE, (0, 1, 2, 3), 0)
    low_grid = all_lows.reshape(devices, pair_count, 1, 1)
    orders = held_orders.reshape(1, 1, slot_count, 1)
    halves = jnp.arange(2, dtype=jnp.int32).reshape(1, 1, 1, 2)
    slot_ids = jnp.arange(slot_count, dtype=jnp.int32).reshape(1, 1, slot_count, 1)
    live = orders >= 0

    def place(position):
        spot = slot_ids * slot_width + 2 * position + halves
        return jnp.where(live, spot, fill_col).reshape(devices, pair_count, -1)

    first = place(jnp.where(orders <= low_grid, low_grid - orders, truncation + 1 - low_grid))
    second = place(truncation - low_grid - orders)
    hit = orders == low_grid
    found = jnp.any(hit, axis=2)
    slot_hit = jnp.sum(jnp.where(hit, slot_ids, 0), axis=2)
    extra = slot_hit * slot_width + 2 * (truncation + 1 - low_grid[:, :, 0]) + halves[:, :, 0]
    extra = jnp.where(found, extra, fill_col)
    column = jnp.concatenate([first, second, extra], axis=2).reshape(-1)
    source_orders = all_orders.reshape(devices, 1, slot_count, 1)
    low_first = jnp.broadcast_to(
        source_orders <= own_low[..., None], (devices, pair_count, slot_count, 2)
    ).reshape(devices, pair_count, -1)
    low_mask = jnp.concatenate(
        [low_first, jnp.zeros((devices, pair_count, 2 * slot_count + 2), jnp.bool_)], axis=2
    )
    split = 2 * slot_count
    per_pair = low_mask.shape[2]
    recv_shape = (devices, pair_count, per_pair)
    divergence = state[:layer_heights_count]
    thermal_state_array = state[layer_heights_count : 2 * layer_heights_count]
    pressure = state[2 * layer_heights_count]
    coeff_index = (jnp.arange(slot_width, dtype=jnp.int32) // 2)[None, :]
    order_col = held_orders[:, None]
    degree = jnp.where(
        coeff_index <= truncation - order_col, order_col + coeff_index, coeff_index - 1
    )
    lap_scale = ((degree * (degree + 1)).astype(jnp.float32) / denom).reshape(-1)
    height_drive_term = jnp.dot(
        height_operator, thermal_state_array, preferred_element_type=jnp.float32
    )
    height_drive_term = (
        height_drive_term
        + pressure_column.astype(jnp.float32)[:, None] * pressure.astype(jnp.float32)[None, :]
    )
    right_side = (divergence.astype(jnp.float32) + lap_scale[None, :] * height_drive_term).astype(
        jnp.bfloat16
    )
    message = jnp.take(right_side, column, axis=1, mode="fill", fill_value=0)
    arriving_arrays = send_out(message).reshape((layer_heights_count,) + recv_shape)
    div_sent = solve_columns(inverses, arriving_arrays, low_mask, split).reshape(
        layer_heights_count, -1
    )
    returned = send_home(div_sent)
    next_spreading_rate = (
        jnp.zeros((layer_heights_count, fill_col), jnp.bfloat16)
        .at[:, column]
        .set(returned, mode="drop")
    )
    next_thermal_state = (
        thermal_state_array.astype(jnp.float32)
        - jnp.dot(thermal_response_matrix, next_spreading_rate, preferred_element_type=jnp.float32)
    ).astype(jnp.bfloat16)
    surface_mass_next = (
        pressure.astype(jnp.float32)
        - jnp.dot(mass_row, next_spreading_rate, preferred_element_type=jnp.float32)
    ).astype(jnp.bfloat16)
    live_slot = jnp.repeat(held_orders >= 0, slot_width)[None, :]
    result = jnp.concatenate(
        [next_spreading_rate, next_thermal_state, surface_mass_next[None, :]], axis=0
    )
    return jnp.where(live_slot, result, jnp.zeros_like(result))


def solution(mesh):
    torus = Mesh(
        mesh.devices.reshape(mesh.shape["grp"], 4, 4, 2), ("grp", "wave_0", "wave_1", "wave_2")
    )
    placed = (
        P(None, GRP_WAVE),
        P(GRP_WAVE),
        P(GRP_WAVE),
        P(GRP_WAVE, None, None, None),
        P(),
        P(),
        P(),
        P(),
    )
    return jax.shard_map(
        shards, mesh=torus, in_specs=placed, out_specs=P(None, GRP_WAVE), check_vma=False
    )
```

profile of v0, /device:TPU:1, one launch (start us, length us, event | category | flops | bytes accessed | tf_op | source)
XLA Modules:
  0.0 343.3 jit_solution(1832600771421519429)
XLA Ops:
  0.0 1.3 dynamic-slice
  2.8 20.8 %all-reduce = s32[192]{0:T(256)S(1)} all-reduce(s32[192]{0:T(256)S(1)} %dynamic-update-slice), channel_id=2, replica_groups=mesh['grp'=4,'wave_0'=4,'wave_1'=4,'wave_2'=2] {'grp','wave_0','wave_1'}, use_global_device_ids=true, to_apply=%add | all-reduce | flops 192 | bytes 1536
  23.8 7.4 %all-gather.2 = s32[2,64,3]{1,2,0:T(4,128)S(1)} all-gather(s32[1,64,3]{1,2,0:T(4,128)S(1)} %copy.56), channel_id=1, replica_groups=mesh['grp'=4,'wave_0'=4,'wave_1'=4,'wave_2'=2] {'wave_2'}, dimensions={0}, use_global_device_ids=true | all-gather | bytes 2304 | tf_op jit(solution)/shard_map/all_gather | solution.py:20
  38.5 3.9 %fusion.4 = bf16[137,7690]{1,0:T(8,128)(2,1)S(1)} fusion(bf16[137,137]{1,0:T(8,128)(2,1)S(1)} %copy-done, f32[7690]{0:T(1024)S(1)} %convert_reduce_fusion, f32[137]{0:T(256)S(1)} %convert_element_type.37, f32[7690]{0:T(1024)S(1)} %fusion.11, bf16[275,7690]{1,0:T(8,128)(2,1)} %param.8), kind=kOutput, calls=%fused_computation.8 | convolution fusion | flops 294988448 | bytes 6704074 | tf_op jit(solution)/shard_map/dot_general | solution.py:111
  42.4 3.7 %copy.67 = bf16[137,7690]{0,1:T(8,128)(2,1)} copy(bf16[137,7690]{1,0:T(8,128)(2,1)S(1)} %fusion.4) | data formatting | bytes 4214120 | tf_op jit(solution)/shard_map/convert_element_type | solution.py:118
  46.1 22.6 %gather_fusion = bf16[8448,137]{1,0:T(8,128)(2,1)} fusion(bf16[137,7690]{0,1:T(8,128)(2,1)} %copy.67, s32[9216]{0:T(1024)S(1)} %pad_clamp_fusion), kind=kCustom, calls=%fused_computation | custom fusion | bytes 4663296 | tf_op jit(solution)/shard_map/jit(_take)/gather | solution.py:121
  68.8 5.0 %copy.68 = bf16[137,8448]{1,0:T(8,128)(2,1)S(1)} copy(bf16[137,8448]{0,1:T(8,128)(2,1)} %bitcast.62) | data formatting | bytes 4629504 | tf_op jit(solution)/shard_map/jit(_take)/gather | solution.py:121
  73.8 16.8 %gather.7 = bf16[137,128,66]{2,1,0:T(8,128)(2,1)} reshape(bf16[137,8448]{1,0:T(8,128)(2,1)S(1)} %copy.68) | data formatting | bytes 4629504 | tf_op jit(solution)/shard_map/jit(_take)/gather | solution.py:121
  90.7 2.6 broadcast_select_fusion
  93.2 5.0 %copy.88 = bf16[137,128,66]{2,0,1:T(8,128)(2,1)} copy(bf16[137,128,66]{2,1,0:T(8,128)(2,1)S(1)} %broadcast_select_fusion) | data formatting | bytes 4629504 | tf_op jit(solution)/shard_map/jit(_take)/select_n | solution.py:121
  98.3 17.0 %reshape.283 = bf16[128,2,4521]{2,1,0:T(2,128)(2,1)} reshape(bf16[128,137,66]{2,1,0:T(8,128)(2,1)} %bitcast.58) | data formatting | bytes 4629504
  115.3 3.9 %all-to-all-start = ((bf16[128,2,4521]{2,1,0:T(2,128)(2,1)}), bf16[128,2,4521]{2,1,0:T(2,128)(2,1)S(1)}, u32[]{:S(2)}, u32[]{:S(2)}) async-start(bf16[128,2,4521]{2,1,0:T(2,128)(2,1)} %reshape.283), calls=%async_computation | async-start | bytes 4718592 | tf_op jit(solution)/shard_map/all_to_all | solution.py:32
  120.9 13.8 %all-reduce.1 = s32[20]{0:T(128)S(1)} all-reduce(s32[20]{0:T(128)S(1)} %dynamic-update-slice.1), channel_id=3, replica_groups=mesh['grp'=4,'wave_0'=4,'wave_1'=4,'wave_2'=2] {'grp'}, use_global_device_ids=true, to_apply=%add.1 | all-reduce | flops 20 | bytes 160
  134.8 15.7 %all-gather.3 = s32[4,4,5]{2,1,0:T(4,128)S(1)} all-gather(s32[1,4,5]{2,1,0:T(4,128)S(1)} %reshape.258), channel_id=1, replica_groups=mesh['grp'=4,'wave_0'=4,'wave_1'=4,'wave_2'=2] {'wave_0'}, dimensions={0}, use_global_device_ids=true | all-gather | bytes 400 | tf_op jit(solution)/shard_map/all_gather | solution.py:20
  150.5 16.4 %all-gather.4 = s32[4,16,5]{1,2,0:T(8,128)S(1)} all-gather(s32[1,16,5]{1,2,0:T(8,128)S(1)} %copy.79), channel_id=1, replica_groups=mesh['grp'=4,'wave_0'=4,'wave_1'=4,'wave_2'=2] {'wave_1'}, dimensions={0}, use_global_device_ids=true | all-gather | bytes 1600 | tf_op jit(solution)/shard_map/all_gather | solution.py:20
  167.0 10.1 %all-gather.5 = s32[2,64,5]{1,2,0:T(8,128)S(1)} all-gather(s32[1,64,5]{1,2,0:T(8,128)S(1)} %reshape.262), channel_id=1, replica_groups=mesh['grp'=4,'wave_0'=4,'wave_1'=4,'wave_2'=2] {'wave_2'}, dimensions={0}, use_global_device_ids=true | all-gather | bytes 3840 | tf_op jit(solution)/shard_map/all_gather | solution.py:20
  177.9 1.3 fusion.16
  179.2 10.2 %reshape.284 = bf16[128,137,66]{2,1,0:T(8,128)(2,1)} reshape(bf16[128,2,4521]{2,1,0:T(2,128)(2,1)S(1)} %all-to-all-done) | data formatting | bytes 4629504
  189.4 6.0 %copy.70 = bf16[137,128,66]{1,0,2:T(8,128)(2,1)S(1)} copy(bf16[137,128,66]{2,0,1:T(8,128)(2,1)} %bitcast.59) | data formatting | bytes 4629504 | tf_op jit(solution)/shard_map/all_to_all | solution.py:32
  197.1 4.9 %copy.73 = bf16[137,128,66]{2,0,1:T(8,128)(2,1)} copy(bf16[137,128,66]{1,0,2:T(8,128)(2,1)S(1)} %bitcast.66) | data formatting | bytes 4629504 | tf_op jit(solution)/shard_map/convert_element_type | solution.py:50
  202.1 16.8 %reshape.285 = bf16[128,2,4521]{2,1,0:T(2,128)(2,1)} reshape(bf16[128,137,66]{2,1,0:T(8,128)(2,1)} %bitcast.60) | data formatting | bytes 4629504
  218.9 5.6 %all-to-all-start.1 = ((bf16[128,2,4521]{2,1,0:T(2,128)(2,1)}), bf16[128,2,4521]{2,1,0:T(2,128)(2,1)S(1)}, u32[]{:S(2)}, u32[]{:S(2)}) async-start(bf16[128,2,4521]{2,1,0:T(2,128)(2,1)} %reshape.285), calls=%async_computation.1 | async-start | bytes 4718592 | tf_op jit(solution)/shard_map/all_to_all | solution.py:36
  224.8 32.9 %all-to-all-done.1 = bf16[128,2,4521]{2,1,0:T(2,128)(2,1)S(1)} async-done(((bf16[128,2,4521]{2,1,0:T(2,128)(2,1)}), bf16[128,2,4521]{2,1,0:T(2,128)(2,1)S(1)}, u32[]{:S(2)}, u32[]{:S(2)}) %all-to-all-start.1) | async-done | bytes 2314784 | tf_op jit(solution)/shard_map/all_to_all | solution.py:36
  257.7 10.2 %reshape.286 = bf16[128,137,66]{2,1,0:T(8,128)(2,1)} reshape(bf16[128,2,4521]{2,1,0:T(2,128)(2,1)S(1)} %all-to-all-done.1) | data formatting | bytes 4629504
  267.9 5.6 %copy.74 = bf16[137,128,66]{2,1,0:T(8,128)(2,1)} copy(bf16[137,128,66]{2,0,1:T(8,128)(2,1)} %bitcast.61) | data formatting | bytes 4629504 | tf_op jit(solution)/shard_map/all_to_all | solution.py:36
  273.5 7.4 %reshape.241 = bf16[137,8448]{1,0:T(8,128)(2,1)S(1)} reshape(bf16[137,128,66]{2,1,0:T(8,128)(2,1)} %copy.74) | data formatting | bytes 4629504 | tf_op jit(solution)/shard_map/all_to_all | solution.py:36
  280.9 3.8 %copy.75 = bf16[8448,137]{1,0:T(8,128)(2,1)} copy(bf16[8448,137]{0,1:T(8,128)(2,1)S(1)} %bitcast.65) | data formatting | bytes 4629504 | tf_op jit(solution)/shard_map/all_to_all | solution.py:36
  284.7 44.6 %scatter_custom_fusion = bf16[137,7690]{0,1:T(8,128)(2,1)} fusion(s32[8448]{0:T(1024)S(1)} %fusion.9, bf16[8448,137]{1,0:T(8,128)(2,1)} %copy.75, bf16[]{:T(256)} %constant.21.clone.1), kind=kCustom, calls=%fused_computation.17 | custom fusion | bytes 2107572 | tf_op jit(solution)/shard_map/scatter | solution.py:130
  329.3 4.6 %copy.76 = bf16[137,7690]{1,0:T(8,128)(2,1)S(1)} copy(bf16[137,7690]{0,1:T(8,128)(2,1)} %scatter_custom_fusion) | data formatting | bytes 4214120 | tf_op jit(solution)/shard_map/scatter | solution.py:130
  334.0 4.5 %fusion.3 = bf16[137,7690]{1,0:T(8,128)(2,1)S(1)} fusion(bf16[137,7690]{0,1:T(8,128)(2,1)} %scatter_custom_fusion, bf16[137,137]{1,0:T(8,128)(2,1)S(1)} %copy-done.7, bf16[275,7690]{1,0:T(8,128)(2,1)} %param.8), kind=kOutput, calls=%fused_computation.7 | convolution fusion | flops 291827840 | bytes 6358718 | tf_op jit(solution)/shard_map/dot_general | solution.py:134
  338.5 1.1 convolution_reduce_fusion
  339.7 3.3 maximum_select_fusion
  (81 shorter events, 12.1 us)
Async XLA Ops:
  0.0 38.5 %copy-start = (bf16[137,137]{1,0:T(8,128)(2,1)S(1)}, bf16[137,137]{1,0:T(8,128)(2,1)}, u32[]{:S(2)}) copy-start(bf16[137,137]{1,0:T(8,128)(2,1)} %param.12) | copy-start | bytes 112618
  115.3 4.0 %copy-start.9 = (u32[128]{0:T(128)S(1)}, u32[128]{0:T(128)}, u32[]{:S(2)}) copy-start(u32[128]{0:T(128)} %constant.72) | copy-start | bytes 1540
  115.3 5.3 %copy-start.5 = (s32[5]{0:T(128)S(1)}, s32[5]{0:T(128)}, u32[]{:S(2)}) copy-start(s32[5]{0:T(128)} %param.9) | copy-start | bytes 64
  115.3 62.4 %copy-start.6 = (s32[3]{0:T(128)S(1)}, s32[3]{0:T(128)}, u32[]{:S(2)}) copy-start(s32[3]{0:T(128)} %param.10) | copy-start | bytes 40
  115.3 62.6 %copy-start.3 = (bf16[3,2,137,137]{3,1,2,0:T(2,128)(2,1)S(1)}, bf16[3,2,137,137]{3,1,2,0:T(2,128)(2,1)}, u32[]{:S(2)}) copy-start(bf16[3,2,137,137]{3,1,2,0:T(2,128)(2,1)} %param.11) | copy-start | bytes 675688
  115.3 63.9 %all-to-all-start = ((bf16[128,2,4521]{2,1,0:T(2,128)(2,1)}), bf16[128,2,4521]{2,1,0:T(2,128)(2,1)S(1)}, u32[]{:S(2)}, u32[]{:S(2)}) async-start(bf16[128,2,4521]{2,1,0:T(2,128)(2,1)} %reshape.283), calls=%async_computation | async-start | bytes 4718592 | tf_op jit(solution)/shard_map/all_to_all | solution.py:32
  195.4 1.0 copy-start.4
  218.9 5.7 %copy-start.8 = (bf16[137]{0:T(256)(128)(2,1)S(1)}, bf16[137]{0:T(256)(128)(2,1)}, u32[]{:S(2)}) copy-start(bf16[137]{0:T(256)(128)(2,1)} %param.15) | copy-start | bytes 826
  218.9 38.8 %all-to-all-start.1 = ((bf16[128,2,4521]{2,1,0:T(2,128)(2,1)}), bf16[128,2,4521]{2,1,0:T(2,128)(2,1)S(1)}, u32[]{:S(2)}, u32[]{:S(2)}) async-start(bf16[128,2,4521]{2,1,0:T(2,128)(2,1)} %reshape.285), calls=%async_computation.1 | async-start | bytes 4718592 | tf_op jit(solution)/shard_map/all_to_all | solution.py:36
  329.3 4.6 %copy-start.7 = (bf16[137,137]{1,0:T(8,128)(2,1)S(1)}, bf16[137,137]{1,0:T(8,128)(2,1)}, u32[]{:S(2)}) copy-start(bf16[137,137]{1,0:T(8,128)(2,1)} %param.14) | copy-start | bytes 112618
  334.0 4.5 %copy-start.2 = (bf16[137,7690]{0,1:T(8,128)(2,1)S(1)}, bf16[137,7690]{0,1:T(8,128)(2,1)}, u32[]{:S(2)}) copy-start(bf16[137,7690]{0,1:T(8,128)(2,1)} %scatter_custom_fusion) | copy-start | bytes 6321184
  339.7 3.4 copy-start.1
where the time goes:
time: 348 us; the launch traced here: 343 us
  local copies, waits for them, and re-layouts  191 us (55%)
  blocking collectives  84.2 us (24%)
  waiting for transfers between devices  32.9 us (9%)
  other arithmetic  12.4 us (4%)
  matrix products  10.8 us (3%)
  starting transfers between devices  9.59 us (3%)
    unnamed x36, local copies, waits for them, and re-layouts  57.9 us
    all_gather x4, blocking collectives, all_blocks(): tiles = lax.all_gather(tiles, axes[k], axis=0, tiled=True)  49.6 us
    scatter x2, local copies, waits for them, and re-layouts, shards(): next_spreading_rate = jnp.zeros((layer_heights_count, fill_col), jnp.bflo...  49.2 us
    gather x3, local copies, waits for them, and re-layouts, shards(): message = jnp.take(right_side, column, axis=1, mode='fill', fill_value=0)  44.4 us
    unnamed x2, blocking collectives  34.6 us
    all_to_all x1, waiting for transfers between devices, send_home(): lax.all_to_all(message, GRP_WAVE, split_axis=1, concat_axis=1, tiled=True)  32.9 us
    all_to_all x3, local copies, waits for them, and re-layouts, send_home(): lax.all_to_all(message, GRP_WAVE, split_axis=1, concat_axis=1, tiled=True)  16.8 us
  transfers between devices with their start and end apart: 2, of which 1 were waited for; matrix products, arithmetic and copies ran while one was open for 1% of the time, Pallas kernels for 0%

commit v1 on v0

--- a/solution.py
+++ b/solution.py
@@ -17,7 +17,11 @@
 def all_blocks(shard, axes, turns):
     tiles = shard[None]
     for k in turns:
-        tiles = lax.all_gather(tiles, axes[k], axis=0, tiled=True)
+        target = axes[k]
+        y = lax.axis_size(target)
+        tall = jnp.stack(y * [tiles])
+        part_now = lax.all_to_all(tall, target, 0, 0)
+        tiles = jnp.concatenate(part_now, axis=0)
     held = [lax.axis_size(axes[k]) for k in reversed(turns)]
     tiles = tiles.reshape(*held, *shard.shape)
     turned = sorted(range(len(turns)), key=lambda place: turns[len(turns) - 1 - place])

time: 348 us -> 336 us (0.966)
  blocking collectives: 84.2 us -> 11.1 us
  waiting for transfers between devices: 32.9 us -> 71.6 us
  starting transfers between devices: 9.59 us -> 32.9 us
    all_gather x4 -> x0, blocking collectives: 49.6 us -> none  [all_blocks(): tiles = lax.all_gather(tiles, axes[k], axis=0, tiled=True)]
    unnamed x2 -> x0, blocking collectives: 34.6 us -> none
    all_to_all x1, waiting for transfers between devices: 0.01 us -> 30.1 us  [send_out(): lax.all_to_all(message, GRP_WAVE, split_axis=1, concat_axis=1, tiled=True)]
    all_to_all x0 -> x4, starting transfers between devices: none -> 21.6 us  [all_blocks(): part_now = lax.all_to_all(tall, target, 0, 0)]
    all_to_all x0 -> x2, blocking collectives: none -> 11.1 us  [all_blocks(): part_now = lax.all_to_all(tall, target, 0, 0)]
    all_to_all x0 -> x4, waiting for transfers between devices: none -> 8.47 us  [all_blocks(): part_now = lax.all_to_all(tall, target, 0, 0)]
    unnamed x36 -> x27, local copies, waits for them, and re-layouts: 57.9 us -> 54.7 us
  transfers between devices with their start and end apart: 2 -> 6, of which waited for: 1 -> 4; matrix products, arithmetic and copies ran while one was open for 1% -> 26% of each run, Pallas kernels for 0% -> 0%
where the time goes in v1:
time: 336 us; the launch traced here: 330 us
  local copies, waits for them, and re-layouts  192 us (57%)
  waiting for transfers between devices  71.6 us (21%)
  starting transfers between devices  32.9 us (10%)
  other arithmetic  11.1 us (3%)
  blocking collectives  11.1 us (3%)
  matrix products  10.9 us (3%)
    unnamed x27, local copies, waits for them, and re-layouts  54.7 us
    scatter x2, local copies, waits for them, and re-layouts, shards(): next_spreading_rate = jnp.zeros((layer_heights_count, fill_col), jnp.bflo...  49.2 us
    gather x3, local copies, waits for them, and re-layouts, shards(): message = jnp.take(right_side, column, axis=1, mode='fill', fill_value=0)  44.4 us
    all_to_all x1, waiting for transfers between devices, send_home(): lax.all_to_all(message, GRP_WAVE, split_axis=1, concat_axis=1, tiled=True)  33 us
    all_to_all x1, waiting for transfers between devices, send_out(): lax.all_to_all(message, GRP_WAVE, split_axis=1, concat_axis=1, tiled=True)  30.1 us
    all_to_all x4, starting transfers between devices, all_blocks(): part_now = lax.all_to_all(tall, target, 0, 0)  21.6 us
    all_to_all x3, local copies, waits for them, and re-layouts, send_home(): lax.all_to_all(message, GRP_WAVE, split_axis=1, concat_axis=1, tiled=True)  16.8 us
    all_to_all x2, blocking collectives, all_blocks(): part_now = lax.all_to_all(tall, target, 0, 0)  11.1 us
  transfers between devices with their start and end apart: 6, of which 4 were waited for; matrix products, arithmetic and copies ran while one was open for 26% of the time, Pallas kernels for 0%

profile of v1, /device:TPU:1, one launch (start us, length us, event | category | flops | bytes accessed | tf_op | source)
XLA Modules:
  0.0 330.4 jit_solution(13178379724418907945)
XLA Ops:
  1.3 5.8 %all-to-all-start.2 = ((s32[4,1,5]{2,1,0:T(1,128)}), s32[4,1,5]{2,1,0:T(1,128)S(1)}, u32[]{:S(2)}, u32[]{:S(2)}) async-start(s32[4,1,5]{2,1,0:T(1,128)} %stack.20), calls=%async_computation.2 | async-start | bytes 4096 | tf_op jit(solution)/shard_map/all_to_all | solution.py:23
  10.3 4.0 %fusion.4 = bf16[137,7690]{1,0:T(8,128)(2,1)S(1)} fusion(bf16[137,137]{1,0:T(8,128)(2,1)S(1)} %copy-done, f32[7690]{0:T(1024)S(1)} %convert_reduce_fusion, f32[137]{0:T(256)S(1)} %convert_element_type.37, f32[7690]{0:T(1024)S(1)} %fusion.11, bf16[275,7690]{1,0:T(8,128)(2,1)} %param.8), kind=kOutput, calls=%fused_computation.8 | convolution fusion | flops 294988448 | bytes 6704074 | tf_op jit(solution)/shard_map/dot_general | solution.py:115
  14.9 4.0 %all-to-all-start.3 = ((s32[4,4,5]{2,1,0:T(4,128)}), s32[4,4,5]{2,1,0:T(4,128)S(1)}, u32[]{:S(2)}, u32[]{:S(2)}) async-start(s32[4,4,5]{2,1,0:T(4,128)} %stack.21), calls=%async_computation.3 | async-start | bytes 16384 | tf_op jit(solution)/shard_map/all_to_all | solution.py:23
  18.9 4.2 %all-to-all-done.3 = s32[4,4,5]{2,1,0:T(4,128)S(1)} async-done(((s32[4,4,5]{2,1,0:T(4,128)}), s32[4,4,5]{2,1,0:T(4,128)S(1)}, u32[]{:S(2)}, u32[]{:S(2)}) %all-to-all-start.3) | async-done | bytes 352 | tf_op jit(solution)/shard_map/all_to_all | solution.py:23
  23.7 8.5 %all-to-all-start = ((s32[64,1,3]{2,1,0:T(1,128)}), s32[64,1,3]{2,1,0:T(1,128)S(1)}, u32[]{:S(2)}, u32[]{:S(2)}) async-start(s32[64,1,3]{2,1,0:T(1,128)} %stack.18), calls=%async_computation | async-start | bytes 65536 | tf_op jit(solution)/shard_map/all_to_all | solution.py:23
  32.4 3.7 %copy.111 = bf16[137,7690]{0,1:T(8,128)(2,1)} copy(bf16[137,7690]{1,0:T(8,128)(2,1)S(1)} %fusion.4) | data formatting | bytes 4214120 | tf_op jit(solution)/shard_map/convert_element_type | solution.py:122
  36.2 4.3 %all-to-all-done = s32[64,1,3]{2,1,0:T(1,128)S(1)} async-done(((s32[64,1,3]{2,1,0:T(1,128)}), s32[64,1,3]{2,1,0:T(1,128)S(1)}, u32[]{:S(2)}, u32[]{:S(2)}) %all-to-all-start) | async-done | bytes 800 | tf_op jit(solution)/shard_map/all_to_all | solution.py:23
  40.7 7.4 %all_to_all.45 = s32[2,1,192]{2,1,0:T(1,128)S(1)} all-to-all(s32[2,1,192]{2,1,0:T(1,128)S(1)} %reshape.257), channel_id=1, replica_groups=mesh['grp'=4,'wave_0'=4,'wave_1'=4,'wave_2'=2] {'wave_2'}, dimensions={0} | all-to-all | bytes 3072 | tf_op jit(solution)/shard_map/all_to_all | solution.py:23
  48.8 3.2 all-to-all-start.4
  54.6 22.6 %gather_fusion = bf16[8448,137]{1,0:T(8,128)(2,1)} fusion(bf16[137,7690]{0,1:T(8,128)(2,1)} %copy.111, s32[9216]{0:T(1024)S(1)} %pad_clamp_fusion), kind=kCustom, calls=%fused_computation | custom fusion | bytes 4663296 | tf_op jit(solution)/shard_map/jit(_take)/gather | solution.py:125
  77.2 5.0 %copy.112 = bf16[137,8448]{1,0:T(8,128)(2,1)S(1)} copy(bf16[137,8448]{0,1:T(8,128)(2,1)} %bitcast.71) | data formatting | bytes 4629504 | tf_op jit(solution)/shard_map/jit(_take)/gather | solution.py:125
  82.2 16.7 %gather.7 = bf16[137,128,66]{2,1,0:T(8,128)(2,1)} reshape(bf16[137,8448]{1,0:T(8,128)(2,1)S(1)} %copy.112) | data formatting | bytes 4629504 | tf_op jit(solution)/shard_map/jit(_take)/gather | solution.py:125
  99.1 2.6 broadcast_select_fusion
  101.7 5.0 %copy.133 = bf16[137,128,66]{2,0,1:T(8,128)(2,1)} copy(bf16[137,128,66]{2,1,0:T(8,128)(2,1)S(1)} %broadcast_select_fusion) | data formatting | bytes 4629504 | tf_op jit(solution)/shard_map/jit(_take)/select_n | solution.py:125
  106.7 17.0 %reshape.259 = bf16[128,2,4521]{2,1,0:T(2,128)(2,1)} reshape(bf16[128,137,66]{2,1,0:T(8,128)(2,1)} %bitcast.67) | data formatting | bytes 4629504
  123.9 3.7 %all_to_all.46 = s32[2,1,320]{2,1,0:T(1,128)S(1)} all-to-all(s32[2,1,320]{2,1,0:T(1,128)S(1)} %reshape.261), channel_id=1, replica_groups=mesh['grp'=4,'wave_0'=4,'wave_1'=4,'wave_2'=2] {'wave_2'}, dimensions={0} | all-to-all | bytes 5120 | tf_op jit(solution)/shard_map/all_to_all | solution.py:23
  127.6 6.2 %all-to-all-start.6 = ((bf16[128,2,4521]{2,1,0:T(2,128)(2,1)}), bf16[128,2,4521]{2,1,0:T(2,128)(2,1)S(1)}, u32[]{:S(2)}, u32[]{:S(2)}) async-start(bf16[128,2,4521]{2,1,0:T(2,128)(2,1)} %reshape.259), calls=%async_computation.6 | async-start | bytes 4718592 | tf_op jit(solution)/shard_map/all_to_all | solution.py:36
  136.5 30.1 %all-to-all-done.6 = bf16[128,2,4521]{2,1,0:T(2,128)(2,1)S(1)} async-done(((bf16[128,2,4521]{2,1,0:T(2,128)(2,1)}), bf16[128,2,4521]{2,1,0:T(2,128)(2,1)S(1)}, u32[]{:S(2)}, u32[]{:S(2)}) %all-to-all-start.6) | async-done | bytes 2314784 | tf_op jit(solution)/shard_map/all_to_all | solution.py:36
  166.7 10.2 %reshape.260 = bf16[128,137,66]{2,1,0:T(8,128)(2,1)} reshape(bf16[128,2,4521]{2,1,0:T(2,128)(2,1)S(1)} %all-to-all-done.6) | data formatting | bytes 4629504
  176.9 6.0 %copy.114 = bf16[137,128,66]{1,0,2:T(8,128)(2,1)S(1)} copy(bf16[137,128,66]{2,0,1:T(8,128)(2,1)} %bitcast.68) | data formatting | bytes 4629504 | tf_op jit(solution)/shard_map/all_to_all | solution.py:36
  184.6 4.9 %copy.117 = bf16[137,128,66]{2,0,1:T(8,128)(2,1)} copy(bf16[137,128,66]{1,0,2:T(8,128)(2,1)S(1)} %bitcast.75) | data formatting | bytes 4629504 | tf_op jit(solution)/shard_map/convert_element_type | solution.py:54
  189.5 16.8 %reshape.263 = bf16[128,2,4521]{2,1,0:T(2,128)(2,1)} reshape(bf16[128,137,66]{2,1,0:T(8,128)(2,1)} %bitcast.69) | data formatting | bytes 4629504
  206.4 5.2 %all-to-all-start.7 = ((bf16[128,2,4521]{2,1,0:T(2,128)(2,1)}), bf16[128,2,4521]{2,1,0:T(2,128)(2,1)S(1)}, u32[]{:S(2)}, u32[]{:S(2)}) async-start(bf16[128,2,4521]{2,1,0:T(2,128)(2,1)} %reshape.263), calls=%async_computation.7 | async-start | bytes 4718592 | tf_op jit(solution)/shard_map/all_to_all | solution.py:40
  211.8 33.0 %all-to-all-done.7 = bf16[128,2,4521]{2,1,0:T(2,128)(2,1)S(1)} async-done(((bf16[128,2,4521]{2,1,0:T(2,128)(2,1)}), bf16[128,2,4521]{2,1,0:T(2,128)(2,1)S(1)}, u32[]{:S(2)}, u32[]{:S(2)}) %all-to-all-start.7) | async-done | bytes 2314784 | tf_op jit(solution)/shard_map/all_to_all | solution.py:40
  244.8 10.2 %reshape.264 = bf16[128,137,66]{2,1,0:T(8,128)(2,1)} reshape(bf16[128,2,4521]{2,1,0:T(2,128)(2,1)S(1)} %all-to-all-done.7) | data formatting | bytes 4629504
  255.0 5.6 %copy.118 = bf16[137,128,66]{2,1,0:T(8,128)(2,1)} copy(bf16[137,128,66]{2,0,1:T(8,128)(2,1)} %bitcast.70) | data formatting | bytes 4629504 | tf_op jit(solution)/shard_map/all_to_all | solution.py:40
  260.7 7.4 %reshape.241 = bf16[137,8448]{1,0:T(8,128)(2,1)S(1)} reshape(bf16[137,128,66]{2,1,0:T(8,128)(2,1)} %copy.118) | data formatting | bytes 4629504 | tf_op jit(solution)/shard_map/all_to_all | solution.py:40
  268.1 3.8 %copy.119 = bf16[8448,137]{1,0:T(8,128)(2,1)} copy(bf16[8448,137]{0,1:T(8,128)(2,1)S(1)} %bitcast.74) | data formatting | bytes 4629504 | tf_op jit(solution)/shard_map/all_to_all | solution.py:40
  271.9 44.6 %scatter_custom_fusion = bf16[137,7690]{0,1:T(8,128)(2,1)} fusion(s32[8448]{0:T(1024)S(1)} %fusion.9, bf16[8448,137]{1,0:T(8,128)(2,1)} %copy.119, bf16[]{:T(256)} %constant.21.clone.1), kind=kCustom, calls=%fused_computation.17 | custom fusion | bytes 2107572 | tf_op jit(solution)/shard_map/scatter | solution.py:134
  316.5 4.6 %copy.120 = bf16[137,7690]{1,0:T(8,128)(2,1)S(1)} copy(bf16[137,7690]{0,1:T(8,128)(2,1)} %scatter_custom_fusion) | data formatting | bytes 4214120 | tf_op jit(solution)/shard_map/scatter | solution.py:134
  321.1 4.5 %fusion.3 = bf16[137,7690]{1,0:T(8,128)(2,1)S(1)} fusion(bf16[137,7690]{0,1:T(8,128)(2,1)} %scatter_custom_fusion, bf16[137,137]{1,0:T(8,128)(2,1)S(1)} %copy-done.7, bf16[275,7690]{1,0:T(8,128)(2,1)} %param.8), kind=kOutput, calls=%fused_computation.7 | convolution fusion | flops 291827840 | bytes 6358718 | tf_op jit(solution)/shard_map/dot_general | solution.py:138
  326.8 3.3 %maximum_select_fusion = bf16[275,7690]{1,0:T(8,128)(2,1)} fusion(bf16[1,7690]{1,0:T(2,128)(2,1)S(1)} %broadcast_in_dim.131, bf16[137,7690]{1,0:T(8,128)(2,1)S(1)} %fusion.3, bf16[137,7690]{1,0:T(8,128)(2,1)S(1)} %copy.120, pred[7690]{0:T(1024)(128)(4,1)S(1)} %broadcast_in_dim.113), kind=kLoop, calls=%fused_computation.10 | loop fusion | flops 14803250 | bytes 8466690 | tf_op jit(solution)/shard_map/jit(_where)/select_n | solution.py:148
  (90 shorter events, 15.3 us)
Async XLA Ops:
  0.0 10.3 %copy-start = (bf16[137,137]{1,0:T(8,128)(2,1)S(1)}, bf16[137,137]{1,0:T(8,128)(2,1)}, u32[]{:S(2)}) copy-start(bf16[137,137]{1,0:T(8,128)(2,1)} %param.12) | copy-start | bytes 112618
  1.3 13.0 %all-to-all-start.2 = ((s32[4,1,5]{2,1,0:T(1,128)}), s32[4,1,5]{2,1,0:T(1,128)S(1)}, u32[]{:S(2)}, u32[]{:S(2)}) async-start(s32[4,1,5]{2,1,0:T(1,128)} %stack.20), calls=%async_computation.2 | async-start | bytes 4096 | tf_op jit(solution)/shard_map/all_to_all | solution.py:23
  10.3 8.6 %copy-start.5 = (s32[5]{0:T(128)S(1)}, s32[5]{0:T(128)}, u32[]{:S(2)}) copy-start(s32[5]{0:T(128)} %param.9) | copy-start | bytes 64
  10.3 12.8 %copy-start.6 = (s32[3]{0:T(128)S(1)}, s32[3]{0:T(128)}, u32[]{:S(2)}) copy-start(s32[3]{0:T(128)} %param.10) | copy-start | bytes 40
  14.9 8.2 %all-to-all-start.3 = ((s32[4,4,5]{2,1,0:T(4,128)}), s32[4,4,5]{2,1,0:T(4,128)S(1)}, u32[]{:S(2)}, u32[]{:S(2)}) async-start(s32[4,4,5]{2,1,0:T(4,128)} %stack.21), calls=%async_computation.3 | async-start | bytes 16384 | tf_op jit(solution)/shard_map/all_to_all | solution.py:23
  23.7 16.9 %all-to-all-start = ((s32[64,1,3]{2,1,0:T(1,128)}), s32[64,1,3]{2,1,0:T(1,128)S(1)}, u32[]{:S(2)}, u32[]{:S(2)}) async-start(s32[64,1,3]{2,1,0:T(1,128)} %stack.18), calls=%async_computation | async-start | bytes 65536 | tf_op jit(solution)/shard_map/all_to_all | solution.py:23
  48.8 75.0 %all-to-all-start.4 = ((s32[4,16,5]{1,2,0:T(8,128)}), s32[4,16,5]{1,2,0:T(8,128)S(1)}, u32[]{:S(2)}, u32[]{:S(2)}) async-start(s32[4,16,5]{1,2,0:T(8,128)} %stack.22), calls=%async_computation.4 | async-start | bytes 32768 | tf_op jit(solution)/shard_map/all_to_all | solution.py:23
  123.7 10.0 %copy-start.3 = (bf16[3,2,137,137]{3,1,2,0:T(2,128)(2,1)S(1)}, bf16[3,2,137,137]{3,1,2,0:T(2,128)(2,1)}, u32[]{:S(2)}) copy-start(bf16[3,2,137,137]{3,1,2,0:T(2,128)(2,1)} %param.11) | copy-start | bytes 675688
  127.6 39.1 %all-to-all-start.6 = ((bf16[128,2,4521]{2,1,0:T(2,128)(2,1)}), bf16[128,2,4521]{2,1,0:T(2,128)(2,1)S(1)}, u32[]{:S(2)}, u32[]{:S(2)}) async-start(bf16[128,2,4521]{2,1,0:T(2,128)(2,1)} %reshape.259), calls=%async_computation.6 | async-start | bytes 4718592 | tf_op jit(solution)/shard_map/all_to_all | solution.py:36
  182.9 1.0 copy-start.4
  206.3 5.2 %copy-start.8 = (bf16[137]{0:T(256)(128)(2,1)S(1)}, bf16[137]{0:T(256)(128)(2,1)}, u32[]{:S(2)}) copy-start(bf16[137]{0:T(256)(128)(2,1)} %param.15) | copy-start | bytes 826
  206.4 38.5 %all-to-all-start.7 = ((bf16[128,2,4521]{2,1,0:T(2,128)(2,1)}), bf16[128,2,4521]{2,1,0:T(2,128)(2,1)S(1)}, u32[]{:S(2)}, u32[]{:S(2)}) async-start(bf16[128,2,4521]{2,1,0:T(2,128)(2,1)} %reshape.263), calls=%async_computation.7 | async-start | bytes 4718592 | tf_op jit(solution)/shard_map/all_to_all | solution.py:40
  316.5 4.6 %copy-start.7 = (bf16[137,137]{1,0:T(8,128)(2,1)S(1)}, bf16[137,137]{1,0:T(8,128)(2,1)}, u32[]{:S(2)}) copy-start(bf16[137,137]{1,0:T(8,128)(2,1)} %param.14) | copy-start | bytes 112618
  321.1 4.5 %copy-start.2 = (bf16[137,7690]{0,1:T(8,128)(2,1)S(1)}, bf16[137,7690]{0,1:T(8,128)(2,1)}, u32[]{:S(2)}) copy-start(bf16[137,7690]{0,1:T(8,128)(2,1)} %scatter_custom_fusion) | copy-start | bytes 6321184
  326.8 3.4 %copy-start.1 = (bf16[137,137]{1,0:T(8,128)(2,1)S(1)}, bf16[137,137]{1,0:T(8,128)(2,1)}, u32[]{:S(2)}) copy-start(bf16[137,137]{1,0:T(8,128)(2,1)} %param.12) | copy-start | bytes 112618
